TPU v7x, 32 devices: a whole 2x2x4 slice. The times are simulated.
32 devices in a mesh: res: 4 (over x, core), blk: 8 (over z, y).
Axes of the slice: x: 2, y: 2, z: 4, core: 2. Of those that a mesh axis runs over, the one named last changes fastest.
Arguments:
- modes: float32 [2, 8, 4194304], P(None, 'res', 'blk'), may hold values from -0.078125 to 0.078125
Outputs:
- product_modes: float32 [2, 8, 4194304], P(None, 'res', 'blk')
All inputs are finite; a program needn't handle non-finite values.
Results may differ from a plain program's by a relative error of at most 0.000098.
Values sent between devices are 32-bit elements; how exact they have to be, the bound alone decides.
A program may use at most 192 MiB of HBM per device.

v0:
```python
import math

import jax
import jax.numpy as jnp
from jax import lax
from jax.sharding import PartitionSpec as P

INNER = 512

high = lax.Precision.HIGH


def turn(numerator, period):
    angle = 2.0 * math.pi / period * (numerator % period).astype(jnp.float32)
    return jnp.cos(angle), jnp.sin(angle)


def times(left, right):
    return (left[0] * right[0] - left[1] * right[1], left[0] * right[1] + left[1] * right[0])


def conj(pair):
    return (pair[0], -pair[1])


def gauss_tables(length, zero):
    rows = lax.broadcasted_iota(jnp.int32, (length, length), 0) + zero
    columns = lax.broadcasted_iota(jnp.int32, (length, length), 1)
    cosine, sine = turn(rows * columns, length)
    return cosine, sine + cosine, sine - cosine


def dot(left, right):
    return jnp.dot(left, right, precision=high)


def forward_dft(multiply, tables, value):
    base = multiply(tables[0], value[0] + value[1])
    return (base - multiply(tables[1], value[1]), base + multiply(tables[2], value[0]))


def backward_dft(multiply, tables, value):
    base = multiply(tables[0], value[0] + value[1])
    return (base + multiply(tables[2], value[1]), base - multiply(tables[1], value[0]))


def from_left(table, value):
    return dot(table, value)


def from_right(table, value):
    return dot(value, table)


def on_device(modes):
    own, width = modes.shape[1:]
    blocks = lax.axis_size("blk")
    residues = lax.axis_size("res")
    block = lax.axis_index("blk")
    residue = lax.axis_index("res")
    narrow = width // blocks
    inner = min(INNER, width // 8)
    outer = width // inner
    eighths = own * residues
    period = residues * 3 * blocks
    padded = period * width
    zero = residue // (16 * residues)

    def swap(value, bit):
        return lax.ppermute(value, "res", [(q, q ^ bit) for q in range(residues)])

    def sections(owners, offset):
        shape = (3, blocks, 2, len(owners), 2, own, blocks)
        ids = [lax.broadcasted_iota(jnp.int32, shape, i) for i in range(7)]
        owner = sum(
            jnp.where(ids[3] == i, o, 0) for i, o in enumerate(owners)
        )
        freq = residues * (3 * ids[1] + ids[0]) + residue
        place = (own * owner + ids[5] + offset) * blocks + ids[6]
        cosine, sine = turn(freq * place, period)
        return jnp.where(ids[2] == ids[4], cosine, jnp.where(ids[2] == 0, -sine, sine))

    outer_tables = gauss_tables(outer, zero)
    inner_tables = gauss_tables(inner, zero)
    row_ids = lax.broadcasted_iota(jnp.int32, (outer, 1), 0) + zero
    column_ids = lax.broadcasted_iota(jnp.int32, (1, inner), 1)
    inner_turn = turn(row_ids * column_ids, width)

    moved_in = lax.all_to_all(
        modes.reshape(2, own, blocks, narrow), "blk", split_axis=2, concat_axis=2, tiled=True
    )
    mine = moved_in.reshape(2 * own * blocks, narrow)
    across = swap(mine, 2)
    beside = swap(mine, 1)
    diagonal = swap(across, 1)
    every = jnp.concatenate([mine, beside, across, diagonal], axis=0)
    order = [residue, residue ^ 1, residue ^ 2, residue ^ 3]
    matrix = sections(order, 0).reshape(3, 2 * blocks, 2 * own * blocks * residues)

    returned = []
    for slab in range(3):
        section = dot(matrix[slab], every).reshape(blocks, 2, narrow // 128, 128)
        back = lax.all_to_all(section, "blk", split_axis=0, concat_axis=0, tiled=True)
        local = (back[:, 0].reshape(outer, inner), back[:, 1].reshape(outer, inner))
        freq = residues * (3 * block + slab) + residue
        row_turn = turn(freq * (inner * row_ids), padded)
        column_turn = turn(freq * column_ids, padded)
        local = times(row_turn, times(column_turn, local))
        local = forward_dft(from_left, outer_tables, local)
        local = times(inner_turn, local)
        local = forward_dft(from_right, inner_tables, local)
        local = (local[0] * local[0] - local[1] * local[1], 2.0 * local[0] * local[1])
        local = backward_dft(from_right, inner_tables, local)
        local = times(conj(inner_turn), local)
        local = backward_dft(from_left, outer_tables, local)
        local = times(conj(row_turn), times(conj(column_turn), local))
        packed = jnp.stack(
            [part.reshape(blocks, narrow // 128, 128) for part in local], axis=1
        )
        moved = lax.all_to_all(packed, "blk", split_axis=0, concat_axis=0, tiled=True)
        returned.append(moved.reshape(2 * blocks, narrow))
    spectrum = jnp.concatenate(returned, axis=0)

    def share(owners):
        table = sections(owners, eighths // 2) * (1.0 / padded)
        table = table.reshape(6 * blocks, 2 * own * blocks * len(owners))
        return lax.dot_general(
            table, spectrum, (((0,), (0,)), ((), ())), precision=high
        )

    half = 2 * own * blocks
    given = swap(share([residue ^ 1, residue ^ 3]), 1)
    kept = share([residue, residue ^ 2])
    given_across = swap(kept[half:] + given[half:], 2)
    total = kept[:half] + given[:half] + given_across
    home = lax.all_to_all(
        total.reshape(2, own, blocks, narrow), "blk", split_axis=2, concat_axis=2, tiled=True
    )
    return home.reshape(2, own, width)


def solution(mesh):
    return jax.shard_map(
        on_device,
        mesh=mesh,
        in_specs=(P(None, "res", "blk"),),
        out_specs=P(None, "res", "blk"),
        check_vma=False,
    )
```

profile of v0, /device:TPU:0, one launch (start us, length us, event | category | flops | bytes accessed | tf_op | source)
XLA Modules:
  0.0 1978.4 jit_solution(4492513196239416173)
XLA Ops:
  4.5 190.2 %all_to_all.40 = f32[2,2,8,65536]{3,1,0,2:T(2,128)S(1)} all-to-all(f32[2,2,8,65536]{3,1,0,2:T(2,128)S(1)} %bitcast.82), channel_id=1, replica_groups=mesh['res'=4,'blk'=8] {'blk'}, dimensions={2} | all-to-all | bytes 16777216 | tf_op jit(solution)/shard_map/all_to_all | solution.py:89
  204.4 179.8 %collective-permute-done.1 = f32[32,65536]{1,0:T(8,128)} collective-permute-done((f32[32,65536]{1,0:T(8,128)}, f32[32,65536]{1,0:T(8,128)}, u32[]{:S(2)}, u32[]{:S(2)}) %collective-permute-start.1) | collective-permute-done | bytes 8388640 | tf_op jit(solution)/shard_map/ppermute | solution.py:70
  397.7 22.7 %maximum_bitcast_fusion = f32[65536,128]{0,1:T(8,128)} fusion(f32[32,65536]{1,0:T(8,128)} %collective-permute-done.2, f32[32,65536]{1,0:T(8,128)} %collective-permute-done.1, f32[32,65536]{1,0:T(8,128)} %collective-permute-done, f32[32,65536]{1,0:T(8,128)} %bitcast.1), kind=kLoop, calls=%fused_computation | loop fusion | flops 25165824 | bytes 67108864 | tf_op jit(solution)/shard_map/dot_general | solution.py:34
  420.5 33.4 %copy.30 = f32[65536,128]{1,0:T(8,128)} copy(f32[65536,128]{0,1:T(8,128)} %maximum_bitcast_fusion) | data formatting | bytes 67108864 | tf_op jit(solution)/shard_map/dot_general | solution.py:34
  453.9 20.5 %fusion.185 = f32[8,2,512,128]{3,0,2,1:T(8,128)} fusion(f32[512,128,128,1]{2,1,0,3:T(8,128)} %bitcast.78, f32[8,2,128,1]{2,0,1,3:T(8,128)S(1)} %reshape.261), kind=kOutput, calls=%fused_computation.204 | convolution fusion | flops 805306368 | bytes 37756928 | tf_op jit(solution)/shard_map/dot_general | solution.py:34
  492.9 20.3 %fusion.183 = f32[8,2,512,128]{3,0,2,1:T(8,128)} fusion(f32[512,128,128,1]{2,1,0,3:T(8,128)} %bitcast.79, f32[8,2,128,1]{2,0,1,3:T(8,128)S(1)} %reshape.263), kind=kOutput, calls=%fused_computation.202 | convolution fusion | flops 805306368 | bytes 37756928 | tf_op jit(solution)/shard_map/dot_general | solution.py:34
  518.2 59.6 %all-to-all-done.1 = f32[8,2,512,128]{3,2,1,0:T(8,128)} async-done(((f32[8,2,512,128]{3,2,1,0:T(8,128)}), f32[8,2,512,128]{3,2,1,0:T(8,128)}, u32[]{:S(2)}, u32[]{:S(2)}) %all-to-all-start.1) | async-done | bytes 4194336 | tf_op jit(solution)/shard_map/all_to_all | solution.py:103
  582.7 20.3 %fusion.181 = f32[8,2,512,128]{3,0,2,1:T(8,128)} fusion(f32[512,128,128,1]{2,1,0,3:T(8,128)} %bitcast.80, f32[8,2,128,1]{2,0,1,3:T(8,128)S(1)} %reshape.264), kind=kOutput, calls=%fused_computation.200 | convolution fusion | flops 805306368 | bytes 37756928 | tf_op jit(solution)/shard_map/dot_general | solution.py:34
  620.7 19.5 fusion.32
  640.2 20.5 %fusion.71 = f32[1024,512]{1,0:T(8,128)S(1)} fusion(f32[1024,512]{1,0:T(8,128)S(1)} %fusion.32, s32[1024]{0:T(1024)S(1)} %iota_add_fusion.2, f32[1024,512]{1,0:T(8,128)S(1)} %multiply_subtract_fusion.48), kind=kOutput, calls=%fused_computation.126 | convolution fusion | flops 3237478400 | bytes 6295552 | tf_op jit(solution)/shard_map/dot_general | solution.py:34
  660.6 20.2 %fusion.89 = f32[1024,512]{1,0:T(8,128)S(1)} fusion(f32[1024,512]{1,0:T(8,128)S(1)} %fusion.32, s32[1024]{0:T(1024)S(1)} %iota_add_fusion.2, f32[1024,512]{1,0:T(8,128)S(1)} %multiply_add_fusion.46), kind=kOutput, calls=%fused_computation.132 | convolution fusion | flops 3237478400 | bytes 6295552 | tf_op jit(solution)/shard_map/dot_general | solution.py:34
  711.0 15.7 convolution_subtract_fusion.5
  742.1 21.2 %fusion.24 = f32[1024,512]{1,0:T(8,128)S(1)} fusion(s32[1024]{0:T(1024)S(1)} %iota_add_fusion.2, f32[1024]{0:T(1024)S(1)} %get-tuple-element.26, f32[1024]{0:T(1024)S(1)} %get-tuple-element.27, f32[1024,512]{1,0:T(8,128)S(1)} %reshape_squeeze.21, f32[512]{0:T(512)S(1)} %get-tuple-element.30, f32[1024,512]{1,0:T(8,128)} %reshape_squeeze.20, ...), kind=kOutput, calls=%fused_computation.64 | convolution fusion | flops 3242721280 | bytes 6307840 | tf_op jit(solution)/shard_map/dot_general | solution.py:34
  764.8 20.5 %fusion.77 = f32[1024,512]{1,0:T(8,128)S(1)} fusion(f32[1024,512]{1,0:T(8,128)S(1)} %fusion.24, s32[1024]{0:T(1024)S(1)} %iota_add_fusion.2, f32[1024,512]{1,0:T(8,128)S(1)} %multiply_subtract_fusion.49), kind=kOutput, calls=%fused_computation.128 | convolution fusion | flops 3237478400 | bytes 6295552 | tf_op jit(solution)/shard_map/dot_general | solution.py:34
  785.3 20.3 %fusion.95 = f32[1024,512]{1,0:T(8,128)S(1)} fusion(f32[1024,512]{1,0:T(8,128)S(1)} %fusion.24, s32[1024]{0:T(1024)S(1)} %iota_add_fusion.2, f32[1024,512]{1,0:T(8,128)S(1)} %multiply_add_fusion.47), kind=kOutput, calls=%fused_computation.134 | convolution fusion | flops 3237478400 | bytes 6295552 | tf_op jit(solution)/shard_map/dot_general | solution.py:34
  954.7 22.6 %fusion.16 = f32[1024,512]{1,0:T(8,128)} fusion(s32[1024]{0:T(1024)S(1)} %iota_add_fusion.2, f32[1024]{0:T(1024)S(1)} %copy-done.20, f32[1024]{0:T(1024)S(1)} %copy-done.15, f32[1024,512]{1,0:T(8,128)S(1)} %reshape_squeeze.23, f32[512]{0:T(512)S(1)} %copy-done.26, f32[1024,512]{1,0:T(8,128)} %reshape_squeeze.22, f32[512]{0:T(512)S(1)} %copy-done.21), kind=kOutput, calls=%fused_computation.42 | convolution fusion | flops 3242721280 | bytes 6307840 | tf_op jit(solution)/shard_map/dot_general | solution.py:34
  981.4 18.9 fusion.26
  1000.3 20.2 %fusion.74 = f32[1024,512]{1,0:T(8,128)S(1)} fusion(f32[1024,512]{1,0:T(8,128)S(1)} %fusion.26, s32[1024]{0:T(1024)S(1)} %iota_add_fusion.2, f32[1024,512]{1,0:T(8,128)S(1)} %copy-done.13), kind=kOutput, calls=%fused_computation.127 | convolution fusion | flops 3237478400 | bytes 6295552 | tf_op jit(solution)/shard_map/dot_general | solution.py:34
  1020.6 23.0 %multiply_subtract_fusion.14 = (f32[1024,512]{1,0:T(8,128)}, f32[1024,512]{1,0:T(8,128)}) fusion(f32[1024]{0:T(1024)S(1)} %copy-done.33, f32[1024]{0:T(1024)S(1)} %copy-done.19, f32[512]{0:T(512)S(1)} %copy-done.37, f32[1024,512]{1,0:T(8,128)S(1)} %fusion.74, f32[512]{0:T(512)S(1)} %copy-done.25, f32[1024,512]{1,0:T(8,128)S(1)} %fusion.26, ...), kind=kOutput, calls=%fused_computation.71 | convolution fusion | flops 3243769856 | bytes 10502144 | tf_op jit(solution)/shard_map/dot_general | solution.py:34
  1058.1 18.5 fusion.18
  1076.6 20.4 %fusion.83 = f32[1024,512]{1,0:T(8,128)S(1)} fusion(f32[1024,512]{1,0:T(8,128)S(1)} %copy-done.43, s32[1024]{0:T(1024)S(1)} %iota_add_fusion.2, f32[1024,512]{1,0:T(8,128)S(1)} %copy-done.8), kind=kOutput, calls=%fused_computation.130 | convolution fusion | flops 3237478400 | bytes 6295552 | tf_op jit(solution)/shard_map/dot_general | solution.py:34
  1097.0 20.0 %fusion.101 = f32[1024,512]{1,0:T(8,128)S(1)} fusion(f32[1024,512]{1,0:T(8,128)S(1)} %copy-done.43, s32[1024]{0:T(1024)S(1)} %iota_add_fusion.2, f32[1024,512]{1,0:T(8,128)S(1)} %copy-done.7), kind=kOutput, calls=%fused_computation.136 | convolution fusion | flops 3237478400 | bytes 6295552 | tf_op jit(solution)/shard_map/dot_general | solution.py:34
  1117.1 20.4 %fusion.80 = f32[1024,512]{1,0:T(8,128)S(1)} fusion(f32[1024,512]{1,0:T(8,128)S(1)} %fusion.18, s32[1024]{0:T(1024)S(1)} %iota_add_fusion.2, f32[1024,512]{1,0:T(8,128)S(1)} %copy-done.10), kind=kOutput, calls=%fused_computation.129 | convolution fusion | flops 3237478400 | bytes 6295552 | tf_op jit(solution)/shard_map/dot_general | solution.py:34
  1137.5 23.4 %multiply_subtract_fusion.7 = (f32[1024,512]{1,0:T(8,128)}, f32[1024,512]{1,0:T(8,128)}) fusion(f32[1024]{0:T(1024)S(1)} %copy-done.32, f32[1024]{0:T(1024)S(1)} %copy-done.17, f32[512]{0:T(512)S(1)} %copy-done.36, f32[1024,512]{1,0:T(8,128)S(1)} %fusion.80, f32[512]{0:T(512)S(1)} %copy-done.23, f32[1024,512]{1,0:T(8,128)S(1)} %fusion.18, ...), kind=kOutput, calls=%fused_computation.49 | convolution fusion | flops 3243769856 | bytes 10502144 | tf_op jit(solution)/shard_map/dot_general | solution.py:34
  1180.7 17.6 convolution_add_fusion.1
  1258.9 18.5 fusion.10
  1277.5 20.4 %fusion.86 = f32[1024,512]{1,0:T(8,128)S(1)} fusion(f32[1024,512]{1,0:T(8,128)S(1)} %fusion.10, s32[1024]{0:T(1024)S(1)} %iota_add_fusion.2, f32[1024,512]{1,0:T(8,128)S(1)} %multiply_add_fusion.45), kind=kOutput, calls=%fused_computation.131 | convolution fusion | flops 3237478400 | bytes 6295552 | tf_op jit(solution)/shard_map/dot_general | solution.py:34
  1297.8 23.0 %multiply_subtract_fusion = (f32[1024,512]{1,0:T(8,128)}, f32[1024,512]{1,0:T(8,128)}) fusion(f32[1024]{0:T(1024)S(1)} %copy-done.31, f32[1024]{0:T(1024)S(1)} %copy-done.15, f32[512]{0:T(512)S(1)} %copy-done.35, f32[1024,512]{1,0:T(8,128)S(1)} %fusion.86, f32[512]{0:T(512)S(1)} %copy-done.21, f32[1024,512]{1,0:T(8,128)S(1)} %fusion.10, ...), kind=kOutput, calls=%fused_computation.27 | convolution fusion | flops 3243769856 | bytes 10502144 | tf_op jit(solution)/shard_map/dot_general | solution.py:34
  1345.3 84.6 %all-to-all-done.4 = f32[8,2,512,128]{3,2,1,0:T(8,128)} async-done(((f32[8,2,512,128]{3,2,1,0:T(8,128)}), f32[8,2,512,128]{3,2,1,0:T(8,128)}, u32[]{:S(2)}, u32[]{:S(2)}) %all-to-all-start.4) | async-done | bytes 4194336 | tf_op jit(solution)/shard_map/all_to_all | solution.py:120
  1441.3 85.9 %all-to-all-done.6 = f32[8,2,512,128]{3,2,1,0:T(8,128)} async-done(((f32[8,2,512,128]{3,2,1,0:T(8,128)}), f32[8,2,512,128]{3,2,1,0:T(8,128)}, u32[]{:S(2)}, u32[]{:S(2)}) %all-to-all-start.6) | async-done | bytes 4194336 | tf_op jit(solution)/shard_map/all_to_all | solution.py:120
  1584.5 181.2 %collective-permute-done.4 = f32[32,65536]{1,0:T(8,128)S(1)} collective-permute-done((f32[32,65536]{1,0:T(8,128)}, f32[32,65536]{1,0:T(8,128)S(1)}, u32[]{:S(2)}, u32[]{:S(2)}) %collective-permute-start.4) | collective-permute-done | bytes 8388640 | tf_op jit(solution)/shard_map/ppermute | solution.py:70
  1787.2 186.4 %all_to_all.41 = f32[2,2,8,65536]{3,1,0,2:T(2,128)S(1)} all-to-all(f32[2,2,8,65536]{3,1,0,2:T(2,128)S(1)} %copy.40), channel_id=1, replica_groups=mesh['res'=4,'blk'=8] {'blk'}, dimensions={2} | all-to-all | bytes 16777216 | tf_op jit(solution)/shard_map/all_to_all | solution.py:136
  (203 shorter events, 487.6 us)
Async XLA Ops:
  202.9 181.3 %collective-permute-start.1 = (f32[32,65536]{1,0:T(8,128)}, f32[32,65536]{1,0:T(8,128)}, u32[]{:S(2)}, u32[]{:S(2)}) collective-permute-start(f32[32,65536]{1,0:T(8,128)} %bitcast.1), channel_id=1, source_target_pairs={{0,16},{8,24},{16,0},{24,8},{1,17},{9,25},{17,1},{25,9},{2,18},{10... | collective-permute-start | bytes 25165832 | tf_op jit(solution)/shard_map/ppermute | solution.py:70
  204.4 182.1 %collective-permute-start = (f32[32,65536]{1,0:T(8,128)}, f32[32,65536]{1,0:T(8,128)}, u32[]{:S(2)}, u32[]{:S(2)}) collective-permute-start(f32[32,65536]{1,0:T(8,128)} %bitcast.1), channel_id=1, source_target_pairs={{0,8},{8,0},{16,24},{24,16},{1,9},{9,1},{17,25},{25,17},{2,10},{10... | collective-permute-start | bytes 25165832 | tf_op jit(solution)/shard_map/ppermute | solution.py:70
  384.2 13.5 collective-permute-start.2
  479.3 98.6 %all-to-all-start.1 = ((f32[8,2,512,128]{3,2,1,0:T(8,128)}), f32[8,2,512,128]{3,2,1,0:T(8,128)}, u32[]{:S(2)}, u32[]{:S(2)}) async-start(f32[8,2,512,128]{3,2,1,0:T(8,128)} %copy.31), calls=%async_computation.1 | async-start | bytes 8388608 | tf_op jit(solution)/shard_map/all_to_all | solution.py:103
  490.0 130.6 %copy-start.24 = (f32[512]{0:T(512)}, f32[512]{0:T(512)S(1)}, u32[]{:S(2)}) copy-start(f32[512]{0:T(512)S(1)} %get-tuple-element.21) | copy-start | bytes 6148
  490.1 274.0 %copy-start.22 = (f32[512]{0:T(512)}, f32[512]{0:T(512)S(1)}, u32[]{:S(2)}) copy-start(f32[512]{0:T(512)S(1)} %get-tuple-element.31) | copy-start | bytes 6148
  491.5 129.2 %copy-start.18 = (f32[1024]{0:T(1024)}, f32[1024]{0:T(1024)S(1)}, u32[]{:S(2)}) copy-start(f32[1024]{0:T(1024)S(1)} %get-tuple-element.23) | copy-start | bytes 12292
  492.2 271.9 %copy-start.16 = (f32[1024]{0:T(1024)}, f32[1024]{0:T(1024)S(1)}, u32[]{:S(2)}) copy-start(f32[1024]{0:T(1024)S(1)} %get-tuple-element.27) | copy-start | bytes 12292
  577.8 148.8 %all-to-all-start.3 = ((f32[8,2,512,128]{3,2,1,0:T(8,128)}), f32[8,2,512,128]{3,2,1,0:T(8,128)}, u32[]{:S(2)}, u32[]{:S(2)}) async-start(f32[8,2,512,128]{3,2,1,0:T(8,128)} %copy.34), calls=%async_computation.3 | async-start | bytes 8388608 | tf_op jit(solution)/shard_map/all_to_all | solution.py:103
  726.6 218.6 %all-to-all-start.5 = ((f32[8,2,512,128]{3,2,1,0:T(8,128)}), f32[8,2,512,128]{3,2,1,0:T(8,128)}, u32[]{:S(2)}, u32[]{:S(2)}) async-start(f32[8,2,512,128]{3,2,1,0:T(8,128)} %copy.37), calls=%async_computation.5 | async-start | bytes 8388608 | tf_op jit(solution)/shard_map/all_to_all | solution.py:103
  742.1 21.2 %copy-start.1 = (f32[1024,512]{1,0:T(8,128)S(1)}, f32[1024,512]{1,0:T(8,128)}, u32[]{:S(2)}) copy-start(f32[1024,512]{1,0:T(8,128)} %reshape_squeeze.20) | copy-start | bytes 6291460
  954.7 22.6 %copy-start.2 = (f32[1024,512]{1,0:T(8,128)S(1)}, f32[1024,512]{1,0:T(8,128)}, u32[]{:S(2)}) copy-start(f32[1024,512]{1,0:T(8,128)} %reshape_squeeze.22) | copy-start | bytes 6291460
  1000.3 20.2 %copy-start.12 = (f32[1024,512]{1,0:T(8,128)S(1)}, f32[1024,512]{1,0:T(8,128)}, u32[]{:S(2)}) copy-start(f32[1024,512]{1,0:T(8,128)} %multiply_subtract_fusion.33.clone.2) | copy-start | bytes 6291460
  1000.3 20.2 %copy-start.19 = (f32[1024]{0:T(1024)S(1)}, f32[1024]{0:T(1024)}, u32[]{:S(2)}) copy-start(f32[1024]{0:T(1024)} %copy-done.18) | copy-start | bytes 12292
  1000.3 20.2 %copy-start.25 = (f32[512]{0:T(512)S(1)}, f32[512]{0:T(512)}, u32[]{:S(2)}) copy-start(f32[512]{0:T(512)} %copy-done.24) | copy-start | bytes 6148
  1000.3 20.2 %copy-start.33 = (f32[1024]{0:T(1024)S(1)}, f32[1024]{0:T(1024)}, u32[]{:S(2)}) copy-start(f32[1024]{0:T(1024)} %get-tuple-element.28) | copy-start | bytes 12292
  1000.3 20.2 %copy-start.37 = (f32[512]{0:T(512)S(1)}, f32[512]{0:T(512)}, u32[]{:S(2)}) copy-start(f32[512]{0:T(512)} %fusion.232) | copy-start | bytes 6148
  1051.8 280.8 %all-to-all-start.2 = ((f32[8,2,512,128]{3,2,1,0:T(8,128)}), f32[8,2,512,128]{3,2,1,0:T(8,128)}, u32[]{:S(2)}, u32[]{:S(2)}) async-start(f32[8,2,512,128]{3,2,1,0:T(8,128)} %pad_maximum_fusion), calls=%async_computation.2 | async-start | bytes 8388608 | tf_op jit(solution)/shard_map/all_to_all | solution.py:120
  1076.6 20.4 %copy-start.7 = (f32[1024,512]{1,0:T(8,128)S(1)}, f32[1024,512]{1,0:T(8,128)}, u32[]{:S(2)}) copy-start(f32[1024,512]{1,0:T(8,128)} %multiply_add_fusion.48) | copy-start | bytes 6291460
  1097.0 63.9 %copy-start.38 = (f32[1024,512]{1,0:T(8,128)}, f32[1024,512]{1,0:T(8,128)S(1)}, u32[]{:S(2)}) copy-start(f32[1024,512]{1,0:T(8,128)S(1)} %fusion.83) | copy-start | bytes 6291460
  1117.0 43.9 %copy-start.40 = (f32[1024,512]{1,0:T(8,128)}, f32[1024,512]{1,0:T(8,128)S(1)}, u32[]{:S(2)}) copy-start(f32[1024,512]{1,0:T(8,128)S(1)} %fusion.101) | copy-start | bytes 6291460
  1117.0 20.4 %copy-start.9 = (f32[1024,512]{1,0:T(8,128)S(1)}, f32[1024,512]{1,0:T(8,128)}, u32[]{:S(2)}) copy-start(f32[1024,512]{1,0:T(8,128)} %multiply_subtract_fusion.35.clone.2) | copy-start | bytes 6291460
  1117.0 20.4 %copy-start.17 = (f32[1024]{0:T(1024)S(1)}, f32[1024]{0:T(1024)}, u32[]{:S(2)}) copy-start(f32[1024]{0:T(1024)} %copy-done.16) | copy-start | bytes 12292
  1117.0 20.4 %copy-start.23 = (f32[512]{0:T(512)S(1)}, f32[512]{0:T(512)}, u32[]{:S(2)}) copy-start(f32[512]{0:T(512)} %copy-done.22) | copy-start | bytes 6148
  1117.0 20.4 %copy-start.32 = (f32[1024]{0:T(1024)S(1)}, f32[1024]{0:T(1024)}, u32[]{:S(2)}) copy-start(f32[1024]{0:T(1024)} %get-tuple-element.29) | copy-start | bytes 12292
  1117.0 20.4 %copy-start.36 = (f32[512]{0:T(512)S(1)}, f32[512]{0:T(512)}, u32[]{:S(2)}) copy-start(f32[512]{0:T(512)} %fusion.233) | copy-start | bytes 6148
  1277.4 20.4 %copy-start.31 = (f32[1024]{0:T(1024)S(1)}, f32[1024]{0:T(1024)}, u32[]{:S(2)}) copy-start(f32[1024]{0:T(1024)} %fusion.225) | copy-start | bytes 12292
  1277.4 20.4 %copy-start.35 = (f32[512]{0:T(512)S(1)}, f32[512]{0:T(512)}, u32[]{:S(2)}) copy-start(f32[512]{0:T(512)} %fusion.234) | copy-start | bytes 6148
  1332.6 97.3 %all-to-all-start.4 = ((f32[8,2,512,128]{3,2,1,0:T(8,128)}), f32[8,2,512,128]{3,2,1,0:T(8,128)}, u32[]{:S(2)}, u32[]{:S(2)}) async-start(f32[8,2,512,128]{3,2,1,0:T(8,128)} %pad_maximum_fusion.1), calls=%async_computation.4 | async-start | bytes 8388608 | tf_op jit(solution)/shard_map/all_to_all | solution.py:120
  1429.9 97.3 %all-to-all-start.6 = ((f32[8,2,512,128]{3,2,1,0:T(8,128)}), f32[8,2,512,128]{3,2,1,0:T(8,128)}, u32[]{:S(2)}, u32[]{:S(2)}) async-start(f32[8,2,512,128]{3,2,1,0:T(8,128)} %pad_maximum_fusion.2), calls=%async_computation.6 | async-start | bytes 8388608 | tf_op jit(solution)/shard_map/all_to_all | solution.py:120
  1547.5 25.5 %collective-permute-start.3 = (f32[64,65536]{1,0:T(8,128)}, f32[64,65536]{1,0:T(8,128)}, u32[]{:S(2)}, u32[]{:S(2)}) collective-permute-start(f32[64,65536]{1,0:T(8,128)} %fusion.143), channel_id=1, source_target_pairs={{0,8},{8,0},{16,24},{24,16},{1,9},{9,1},{17,25},{25,17},{2,10},{10... | collective-permute-start | bytes 50331656 | tf_op jit(solution)/shard_map/ppermute | solution.py:70
  1583.0 182.7 %collective-permute-start.4 = (f32[32,65536]{1,0:T(8,128)}, f32[32,65536]{1,0:T(8,128)S(1)}, u32[]{:S(2)}, u32[]{:S(2)}) collective-permute-start(f32[32,65536]{1,0:T(8,128)} %slice_add_fusion), channel_id=1, source_target_pairs={{0,16},{8,24},{16,0},{24,8},{1,17},{9,25},{17,1},{25,9},{2,18},{10... | collective-permute-start | bytes 25165832 | tf_op jit(solution)/shard_map/ppermute | solution.py:70
  (23 other events, 222.3 us)
where the time goes:
time: 1990 us; the launch traced here: 1980 us
  matrix products  651 us (33%)
  waiting for transfers between devices  614 us (31%)
  blocking collectives  377 us (19%)
  other arithmetic  153 us (8%)
  local copies, waits for them, and re-layouts  147 us (7%)
  starting transfers between devices  35.7 us (2%)
    dot_general x39, matrix products, dot(): return jnp.dot(left, right, precision=high)  624 us
    ppermute x5, waiting for transfers between devices, swap(): return lax.ppermute(value, 'res', [(q, q ^ bit) for q in range(residues)])  384 us
    all_to_all x1, blocking collectives, on_device(): lax.all_to_all(modes.reshape(2, own, blocks, narrow), 'blk', split_axis=2...  190 us
    all_to_all x1, blocking collectives, on_device(): lax.all_to_all(total.reshape(2, own, blocks, narrow), 'blk', split_axis=2...  186 us
    all_to_all x3, waiting for transfers between devices, on_device(): lax.all_to_all(packed, 'blk', split_axis=0, concat_axis=0, tiled=True)  171 us
    dot_general x13, other arithmetic, dot(): return jnp.dot(left, right, precision=high)  90.1 us
    all_to_all x3, waiting for transfers between devices, on_device(): lax.all_to_all(section, 'blk', split_axis=0, concat_axis=0, tiled=True)  59.6 us
    dot_general x7, local copies, waits for them, and re-layouts, dot(): return jnp.dot(left, right, precision=high)  49 us
  transfers between devices with their start and end apart: 11, of which 7 were waited for; matrix products, arithmetic and copies ran while one was open for 35% of the time, Pallas kernels for 0%

commit v1 on v0

v1 whole, which is shorter than its diff:
```python
import functools
import math

import jax
import jax.numpy as jnp
import ml_dtypes
import numpy as np
from jax import lax
from jax.experimental import pallas as pl
from jax.experimental.pallas import tpu as pltpu
from jax.sharding import PartitionSpec as P

AXES = ("res", "blk")
ROWS = 8
UNITS = 4
TILE = 256
VMEM = 60 * 1024 * 1024


def split(value):
    high = value.astype(jnp.bfloat16)
    return high, (value - high.astype(jnp.float32)).astype(jnp.bfloat16)


def host_split(table):
    high = table.astype(ml_dtypes.bfloat16)
    return np.stack([high, (table - high.astype(np.float64)).astype(ml_dtypes.bfloat16)])


def host_turn(left, right, period):
    angle = 2.0 * math.pi / period * ((left[:, None] * right[None, :]) % period)
    return np.cos(angle), np.sin(angle)


def dot(left, right):
    return jnp.dot(left, right, preferred_element_type=jnp.float32)


def dot3(left, right):
    return dot(left[0], right[0]) + dot(left[1], right[0]) + dot(left[0], right[1])


def columns(ref, part, first, lanes, own, high):
    stride = ref.shape[1] // high
    starts = [(first + i) * own + pl.program_id(1) for i in range(lanes)]
    return [(part, pl.ds(start, high, stride=stride)) for start in starts]


def forward_kernel(tile, own, x_ref, m_ref, w_ref, t_ref, o_ref, l_ref):
    high, low = m_ref.shape[3], t_ref.shape[3]
    rows = m_ref.shape[2] // 2
    lanes = tile // 128

    def first(j, _):
        at = pl.ds(pl.multiple_of(j * tile, tile), tile)
        m = (m_ref[0, 0], m_ref[0, 1])
        real, imag = [
            dot3(m, split(jnp.concatenate(
                [x_ref[p, r, :] for p, r in columns(x_ref, part, j * lanes, lanes, own, high)], axis=1
            )))
            for part in range(2)
        ]
        re, im = real[:rows] - imag[rows:], imag[:rows] + real[rows:]
        cos, sin = w_ref[0, 0, :, at], w_ref[0, 1, :, at]
        l_ref[0, :rows, at], l_ref[1, :rows, at] = split(re * cos - im * sin)
        l_ref[0, rows:, at], l_ref[1, rows:, at] = split(re * sin + im * cos)
        return 0

    def second(j, _):
        at = pl.ds(pl.multiple_of(j * tile, tile), tile)
        value = (l_ref[0], l_ref[1])
        by_cos = dot3(value, (t_ref[0, 0, :, at], t_ref[0, 1, :, at]))
        by_sin = dot3(value, (t_ref[1, 0, :, at], t_ref[1, 1, :, at]))
        shape = (rows // ROWS, ROWS, tile)
        o_ref[:, 0, 0, :, at] = (by_cos[:rows] - by_sin[rows:]).reshape(shape)
        o_ref[:, 0, 1, :, at] = (by_sin[:rows] + by_cos[rows:]).reshape(shape)
        return 0

    lax.fori_loop(0, low // tile, first, 0)
    lax.fori_loop(0, low // tile, second, 0)


def inverse_kernel(tile, own, units, x_ref, m_ref, w_ref, t_ref, *rest):
    a_ref, o_ref, l_ref = rest if len(rest) == 3 else (None, *rest)
    high, low = m_ref.shape[2], t_ref.shape[3]
    rows = x_ref.shape[0] * ROWS
    lanes = tile // 128
    for part in range(2):
        value = split(x_ref[:, 0, part].reshape(rows, low))
        l_ref[0, part * rows:(part + 1) * rows], l_ref[1, part * rows:(part + 1) * rows] = value

    def column(j, _):
        at = pl.ds(pl.multiple_of(j * tile, tile), tile)
        value = (l_ref[0], l_ref[1])
        by_cos = dot3(value, (t_ref[0, 0, :, at], t_ref[0, 1, :, at]))
        by_sin = dot3(value, (t_ref[1, 0, :, at], t_ref[1, 1, :, at]))
        re, im = by_cos[:rows] + by_sin[rows:], by_cos[rows:] - by_sin[:rows]
        cos, sin = w_ref[0, 0, :, at], w_ref[0, 1, :, at]
        re, im = re * cos + im * sin, im * cos - re * sin
        m = (m_ref[0, 0], m_ref[0, 1])
        real = dot3(m, split(jnp.concatenate([re, im], axis=0)))
        imag = dot3(m, split(jnp.concatenate([im, -re], axis=0)))
        for part, value in enumerate((real, imag)):
            for i, (p, r) in enumerate(columns(o_ref, part, j * lanes, lanes, own, high)):
                now = value[:, i * 128:(i + 1) * 128]
                before = 0.0 if a_ref is None else a_ref[p, r, :]
                if units > 1:
                    before = jnp.where(pl.program_id(0) == 0, before, o_ref[p, r, :])
                o_ref[p, r, :] = now + before
        return 0

    lax.fori_loop(0, low // tile, column, 0)


def rotate(value, step, period, scale=1.0):
    re, im = value
    step %= period
    if (4 * step) % period == 0:
        turns = (4 * step) // period
        re, im = [(re, im), (-im, re), (-re, -im), (im, -re)][turns]
        return (re, im) if scale == 1.0 else (re * scale, im * scale)
    angle = 2.0 * math.pi * step / period
    cos, sin = math.cos(angle) * scale, math.sin(angle) * scale
    if (8 * step) % period == 0:
        root = math.sqrt(0.5) * scale
        plus, minus = (re + im) * root, (re - im) * root
        return {1: (minus, plus), 3: (-plus, minus), 5: (-minus, -plus), 7: (plus, -minus)}[(8 * step) // period]
    return re * cos - im * sin, re * sin + im * cos


def add(a, b):
    return a[0] + b[0], a[1] + b[1]


def sub(a, b):
    return a[0] - b[0], a[1] - b[1]


def small_dft(values, sign):
    n = len(values)
    if n == 1:
        return values
    if n % 4:
        return [add(values[0], values[1]), sub(values[0], values[1])]
    q = n // 4
    parts = [[], [], [], []]
    for i in range(q):
        a, b, c, d = values[i], values[i + q], values[i + 2 * q], values[i + 3 * q]
        s, t, u, v = add(a, c), sub(a, c), add(b, d), rotate(sub(b, d), sign, 4)
        parts[0].append(add(s, u))
        parts[1].append(rotate(add(t, v), sign * i, n))
        parts[2].append(rotate(sub(s, u), 2 * sign * i, n))
        parts[3].append(rotate(sub(t, v), 3 * sign * i, n))
    done = [small_dft(part, sign) for part in parts]
    return [done[i % 4][i // 4] for i in range(n)]


def square_kernel(blocks, start, scale, x_ref, o_ref):
    sign = (1 - 2 * ((start + pl.program_id(0)) % 2)).astype(jnp.float32)
    owners, own = x_ref.shape[:2]
    count = owners * own
    half = count // 2
    period = 3 * half

    def place(q):
        eighth, block = divmod(q, blocks)
        return (eighth // own) * blocks + block, eighth % own

    def load(q):
        owner, e = place(q)
        return x_ref[owner, e, 0], x_ref[owner, e, 1]

    third = []
    for rho in range(3):
        folded = [
            rotate(add(load(q), rotate(load(q + half), rho, 3)), rho * q, period) for q in range(half)
        ]
        values = small_dft(folded, 1)
        values = [(re * re - im * im, 2.0 * (re * im)) for re, im in values]
        values = small_dft(values, -1)
        third.append([rotate(value, -rho * q, period) for q, value in enumerate(values)])

    def coefficient(c):
        q, s = c % half, c // half
        total = third[0][q]
        for rho in (1, 2):
            total = add(total, rotate(third[rho][q], -rho * s, 3))
        return total

    before = coefficient(half - 1)
    for c in range(half, 3 * half):
        now = coefficient(c)
        both = now[0] + sign * before[0], now[1] + sign * before[1]
        owner, e = place(c - half)
        o_ref[owner, e, 0] = both[0] * scale
        o_ref[owner, e, 1] = both[1] * scale
        before = now


def on_device(modes):
    own, width = modes.shape[1:]
    blocks = lax.axis_size("blk")
    devices = blocks * lax.axis_size("res")
    units = UNITS
    while units > 2 and width // (devices * ROWS * units // 2) < 128:
        units //= 2
    rows = devices * ROWS
    high = rows * units // 2
    low = width // high
    tile = min(TILE, low)

    highs, lows = np.arange(high), np.arange(low)
    low_tables = np.stack([host_split(table) for table in host_turn(lows, lows, low)])
    twiddles, befores, afters = [], [], []
    for unit in range(units):
        freq = 2 * (unit // 2 * rows + np.arange(rows)) + unit % 2
        twiddles.append(np.stack(host_turn(freq, lows, 2 * width)).astype(np.float32))
        cos, sin = host_turn(freq, highs, 2 * high)
        befores.append(host_split(np.concatenate([cos, sin], axis=0)))
        afters.append(host_split(np.concatenate([cos.T, sin.T], axis=1)))
    low_tables, twiddles, befores, afters = [
        jnp.asarray(a) for a in (low_tables, np.stack(twiddles), np.stack(befores), np.stack(afters))
    ]

    once = pl.Buffered(1)
    tables = pl.BlockSpec(low_tables.shape, lambda u, e: (0, 0, 0, 0), pipeline_mode=once)
    field = (2, own * width // 128, 128)
    fields = pl.BlockSpec(field, lambda u, e: (0, 0, 0), pipeline_mode=once)
    packet = pl.BlockSpec((devices, 1, 2, ROWS, low), lambda u, e: (0, e, 0, u, 0))
    params = pltpu.CompilerParams(vmem_limit_bytes=VMEM)
    scratch = [pltpu.VMEM((2, 2 * rows, low), jnp.bfloat16)]

    def of_unit(start, table):
        return pl.BlockSpec((1, *table.shape[1:]), lambda u, e: (start + u, 0, 0, 0))

    def message(count):
        return jax.ShapeDtypeStruct((devices, own, 2, count * ROWS, low), jnp.float32)

    def cost(count):
        flops = count * own * 3 * 8 * rows * low * (high + low)
        return pl.CostEstimate(flops=flops, bytes_accessed=8 * own * width, transcendentals=0)

    def forward(start, count, field_in):
        return pl.pallas_call(
            functools.partial(forward_kernel, tile, own),
            out_shape=message(count),
            grid=(count, own),
            in_specs=[fields, of_unit(start, befores), of_unit(start, twiddles), tables],
            out_specs=packet,
            scratch_shapes=scratch,
            compiler_params=params,
            cost_estimate=cost(count),
            name="forward",
        )(field_in, befores, twiddles, low_tables)

    def inverse(start, count, packets, total):
        extra = [] if total is None else [total]
        return pl.pallas_call(
            functools.partial(inverse_kernel, tile, own, count),
            out_shape=jax.ShapeDtypeStruct(field, jnp.float32),
            grid=(count, own),
            in_specs=[packet, of_unit(start, afters), of_unit(start, twiddles), tables, *([fields] * len(extra))],
            out_specs=pl.BlockSpec(field, lambda u, e: (0, 0, 0)),
            scratch_shapes=scratch,
            compiler_params=params,
            cost_estimate=cost(count),
            name="inverse",
        )(packets, afters, twiddles, low_tables, *extra)

    def square(start, offset, count, packets):
        def lanes(skip):
            return pl.BlockSpec((devices, own, 2, ROWS, 128), lambda u, j: (0, 0, 0, skip + u, j))

        scale = 1.0 / (3 * devices * own * width)
        return pl.pallas_call(
            functools.partial(square_kernel, blocks, start + offset, scale),
            out_shape=message(count),
            grid=(count, low // 128),
            in_specs=[lanes(offset)],
            out_specs=lanes(0),
            compiler_params=params,
            cost_estimate=cost(count),
            name="square",
        )(packets)

    def exchange(packets):
        return lax.all_to_all(packets, AXES, split_axis=0, concat_axis=0, tiled=True)

    field_in = modes.reshape(2, own, width // 128, 128).transpose(0, 2, 1, 3).reshape(field)
    rest = units - 1
    first = exchange(forward(0, 1, field_in))
    second = exchange(forward(1, rest, field_in))
    home = exchange(square(0, 0, 1, first))
    if rest > 1:
        middle = exchange(square(1, 0, rest - 1, second))
    last = square(1, rest - 1, 1, second)
    total = inverse(0, 1, home, None)
    last, total = lax.optimization_barrier((last, total))
    last = exchange(last)
    if rest > 1:
        total = inverse(1, rest - 1, middle, total)
    total = inverse(rest, 1, last, total)
    total = total.reshape(2, width // 128, own, 128).transpose(0, 2, 1, 3)
    return total.reshape(2, own, width)


def solution(mesh):
    return jax.shard_map(
        on_device,
        mesh=mesh,
        in_specs=(P(None, "res", "blk"),),
        out_specs=P(None, "res", "blk"),
        check_vma=False,
    )
```

time: 1990 us -> 864 us (0.43)
  matrix products: 651 us -> 0 us
  blocking collectives: 377 us -> 0 us
  Pallas kernels: 0 us -> 338 us
  other arithmetic: 153 us -> 0 us
  local copies, waits for them, and re-layouts: 147 us -> 0 us
  waiting for transfers between devices: 614 us -> 503 us
    dot_general x41 -> x0, matrix products: 651 us -> none  [the longest x39 624 us: dot(): return jnp.dot(left, right, precision=high)]
    ppermute x5 -> x0, waiting for transfers between devices: 384 us -> none  [swap(): return lax.ppermute(value, 'res', [(q, q ^ bit) for q in range(residues)])]
    all_to_all x2 -> x0, blocking collectives: 377 us -> none  [the longest x1 190 us: on_device(): lax.all_to_all(modes.reshape(2, own, blocks, narrow), 'blk', split_axis=2...]
    pallas_call x0 -> x8, Pallas kernels: none -> 338 us  [the longest x3 183 us: inverse(): pl.pallas_call(functools.partial(inverse_kernel, tile, own, count), out_s...]
    all_to_all x6 -> x5, waiting for transfers between devices: 230 us -> 503 us  [exchange(): lax.all_to_all(packets, AXES, split_axis=0, concat_axis=0, tiled=True)]
    dot_general x13 -> x0, other arithmetic: 90.1 us -> none  [dot(): return jnp.dot(left, right, precision=high)]
    dot_general x7 -> x0, local copies, waits for them, and re-layouts: 49 us -> none  [dot(): return jnp.dot(left, right, precision=high)]
    sub x3 -> x0, other arithmetic: 28.9 us -> none  [times(): left[0] * right[0] - left[1] * right[1]]
  transfers between devices with their start and end apart: 11 -> 5, of which waited for: 7 -> 5; matrix products, arithmetic and copies ran while one was open for 35% -> 0% of each run, Pallas kernels for 0% -> 30%
where the time goes in v1:
time: 864 us; the launch traced here: 863 us
  waiting for transfers between devices  503 us (58%)
  Pallas kernels  338 us (39%)
  starting transfers between devices  22.2 us (3%)
    all_to_all x5, waiting for transfers between devices, exchange(): lax.all_to_all(packets, AXES, split_axis=0, concat_axis=0, tiled=True)  503 us
    pallas_call x3, Pallas kernels, inverse(): pl.pallas_call(functools.partial(inverse_kernel, tile, own, count), out_s...  183 us
    pallas_call x2, Pallas kernels, forward(): pl.pallas_call(functools.partial(forward_kernel, tile, own), out_shape=me...  115 us
    pallas_call x3, Pallas kernels, square(): pl.pallas_call(functools.partial(square_kernel, blocks, start + offset, s...  39.3 us
    all_to_all x5, starting transfers between devices, exchange(): lax.all_to_all(packets, AXES, split_axis=0, concat_axis=0, tiled=True)  22.2 us
  transfers between devices with their start and end apart: 5, of which 5 were waited for; matrix products, arithmetic and copies ran while one was open for 0% of the time, Pallas kernels for 30%

profile of v1, /device:TPU:0, one launch (start us, length us, event | category | flops | bytes accessed | tf_op | source)
XLA Modules:
  0.0 863.0 jit_solution(2331795757324857177)
XLA Ops:
  0.0 32.6 %forward.3 = f32[32,2,2,8,1024]{4,3,2,1,0:T(8,128)} custom-call(f32[2,8192,128]{2,1,0:T(8,128)} %bitcast.10, bf16[4,2,512,512]{3,2,1,0:T(8,128)(2,1)} %constant.10.clone.m_ref, f32[4,2,256,1024]{3,2,1,0:T(8,128)} %constant.9.clone.w_ref, bf16[2,2,1024,1024]{3,2,1,0:T(8,128)(2,1)} %constant.8.clone.t_ref), custom_call_target="tpu_custom_call" | custom-call | flops 19327352832 | bytes 8388608 | tf_op jit(solution)/shard_map/forward/pallas_call | solution.py:244
  32.6 7.5 all-to-all-start.1
  40.1 82.6 %forward.2 = f32[32,2,2,24,1024]{4,3,2,1,0:T(8,128)} custom-call(f32[2,8192,128]{2,1,0:T(8,128)} %bitcast.11, bf16[4,2,512,512]{3,2,1,0:T(8,128)(2,1)} %constant.10.clone.m_ref, f32[4,2,256,1024]{3,2,1,0:T(8,128)} %constant.9.clone.w_ref, bf16[2,2,1024,1024]{3,2,1,0:T(8,128)(2,1)} %constant.8.clone.t_ref), custom_call_target="tpu_custom_call" | custom-call | flops 57982058496 | bytes 8388608 | tf_op jit(solution)/shard_map/forward/pallas_call | solution.py:244
  122.7 13.2 %all-to-all-done.1.x_ref = f32[32,2,2,8,1024]{4,3,2,1,0:T(8,128)} async-done(((f32[32,2,2,8,1024]{4,3,2,1,0:T(8,128)}), f32[32,2,2,8,1024]{4,3,2,1,0:T(8,128)}, u32[]{:S(2)}, u32[]{:S(2)}) %all-to-all-start.1) | async-done | bytes 4194336 | tf_op jit(solution)/shard_map/all_to_all | solution.py:287
  135.8 3.8 all-to-all-start
  139.6 10.1 %square.4 = f32[32,2,2,8,1024]{4,3,2,1,0:T(8,128)} custom-call(f32[32,2,2,8,1024]{4,3,2,1,0:T(8,128)} %all-to-all-done.1.x_ref), custom_call_target="tpu_custom_call" | custom-call | flops 19327352832 | bytes 8388608 | tf_op jit(solution)/shard_map/square/pallas_call | solution.py:275
  149.7 272.4 %all-to-all-done.x_ref = f32[32,2,2,24,1024]{4,3,2,1,0:T(8,128)} async-done(((f32[32,2,2,24,1024]{4,3,2,1,0:T(8,128)}), f32[32,2,2,24,1024]{4,3,2,1,0:T(8,128)}, u32[]{:S(2)}, u32[]{:S(2)}) %all-to-all-start) | async-done | bytes 12582944 | tf_op jit(solution)/shard_map/all_to_all | solution.py:287
  422.1 3.6 all-to-all-start.2
  425.7 18.9 %square.5 = f32[32,2,2,16,1024]{4,3,2,1,0:T(8,128)} custom-call(f32[32,2,2,24,1024]{4,3,2,1,0:T(8,128)} %all-to-all-done.x_ref), custom_call_target="tpu_custom_call" | custom-call | flops 38654705664 | bytes 8388608 | tf_op jit(solution)/shard_map/square/pallas_call | solution.py:275
  444.6 76.9 %all-to-all-done.2.x_ref = f32[32,2,2,8,1024]{4,3,2,1,0:T(8,128)} async-done(((f32[32,2,2,8,1024]{4,3,2,1,0:T(8,128)}), f32[32,2,2,8,1024]{4,3,2,1,0:T(8,128)}, u32[]{:S(2)}, u32[]{:S(2)}) %all-to-all-start.2) | async-done | bytes 4194336 | tf_op jit(solution)/shard_map/all_to_all | solution.py:287
  521.4 3.7 all-to-all-start.4
  525.1 44.8 %inverse.3.rest_0_ = f32[2,8192,128]{2,1,0:T(8,128)} custom-call(f32[32,2,2,8,1024]{4,3,2,1,0:T(8,128)} %all-to-all-done.2.x_ref, bf16[4,2,512,512]{3,2,1,0:T(8,128)(2,1)} %constant.11.clone.m_ref, f32[4,2,256,1024]{3,2,1,0:T(8,128)} %constant.9.clone.w_ref, bf16[2,2,1024,1024]{3,2,1,0:T(8,128)(2,1)} %constant.8.clone.t_ref), custom_call_target="tpu_custom_call" | custom-call | flops 19327352832 | bytes 8388608 | tf_op jit(solution)/shard_map/inverse/pallas_call | solution.py:258
  569.9 10.2 %square.3 = f32[32,2,2,8,1024]{4,3,2,1,0:T(8,128)} custom-call(f32[32,2,2,24,1024]{4,3,2,1,0:T(8,128)} %all-to-all-done.x_ref), custom_call_target="tpu_custom_call" | custom-call | flops 19327352832 | bytes 8388608 | tf_op jit(solution)/shard_map/square/pallas_call | solution.py:275
  580.2 134.6 %all-to-all-done.4.x_ref = f32[32,2,2,16,1024]{4,3,2,1,0:T(8,128)} async-done(((f32[32,2,2,16,1024]{4,3,2,1,0:T(8,128)}), f32[32,2,2,16,1024]{4,3,2,1,0:T(8,128)}, u32[]{:S(2)}, u32[]{:S(2)}) %all-to-all-start.4) | async-done | bytes 8388640 | tf_op jit(solution)/shard_map/all_to_all | solution.py:287
  714.8 3.8 all-to-all-start.3
  718.5 89.4 %inverse.4.rest_0_ = f32[2,8192,128]{2,1,0:T(8,128)} custom-call(f32[32,2,2,16,1024]{4,3,2,1,0:T(8,128)} %all-to-all-done.4.x_ref, bf16[4,2,512,512]{3,2,1,0:T(8,128)(2,1)} %constant.11.clone.m_ref, f32[4,2,256,1024]{3,2,1,0:T(8,128)} %constant.9.clone.w_ref, bf16[2,2,1024,1024]{3,2,1,0:T(8,128)(2,1)} %constant.8.clone.t_ref, f32[2,8192,128]{2,1,0:T(8,128)} %inverse.3.rest_0_), custom_call_target="tpu_custom_call" | custom-call | flops 38654705664 | bytes 8388608 | tf_op jit(solution)/shard_map/inverse/pallas_call | solution.py:258
  807.9 6.2 all-to-all-done.3.x_ref
  814.1 48.9 %inverse.5 = f32[2,8192,128]{2,1,0:T(8,128)} custom-call(f32[32,2,2,8,1024]{4,3,2,1,0:T(8,128)} %all-to-all-done.3.x_ref, bf16[4,2,512,512]{3,2,1,0:T(8,128)(2,1)} %constant.11.clone.m_ref, f32[4,2,256,1024]{3,2,1,0:T(8,128)} %constant.9.clone.w_ref, bf16[2,2,1024,1024]{3,2,1,0:T(8,128)(2,1)} %constant.8.clone.t_ref, f32[2,8192,128]{2,1,0:T(8,128)} %inverse.4.rest_0_), custom_call_target="tpu_custom_call" | custom-call | flops 19327352832 | bytes 8388608 | tf_op jit(solution)/shard_map/inverse/pallas_call | solution.py:258
Async XLA Ops:
  32.6 103.2 %all-to-all-start.1 = ((f32[32,2,2,8,1024]{4,3,2,1,0:T(8,128)}), f32[32,2,2,8,1024]{4,3,2,1,0:T(8,128)}, u32[]{:S(2)}, u32[]{:S(2)}) async-start(f32[32,2,2,8,1024]{4,3,2,1,0:T(8,128)} %forward.3), calls=%async_computation.1 | async-start | bytes 8388608 | tf_op jit(solution)/shard_map/all_to_all | solution.py:287
  135.8 286.3 %all-to-all-start = ((f32[32,2,2,24,1024]{4,3,2,1,0:T(8,128)}), f32[32,2,2,24,1024]{4,3,2,1,0:T(8,128)}, u32[]{:S(2)}, u32[]{:S(2)}) async-start(f32[32,2,2,24,1024]{4,3,2,1,0:T(8,128)} %forward.2), calls=%async_computation | async-start | bytes 25165824 | tf_op jit(solution)/shard_map/all_to_all | solution.py:287
  422.1 99.3 %all-to-all-start.2 = ((f32[32,2,2,8,1024]{4,3,2,1,0:T(8,128)}), f32[32,2,2,8,1024]{4,3,2,1,0:T(8,128)}, u32[]{:S(2)}, u32[]{:S(2)}) async-start(f32[32,2,2,8,1024]{4,3,2,1,0:T(8,128)} %square.4), calls=%async_computation.2 | async-start | bytes 8388608 | tf_op jit(solution)/shard_map/all_to_all | solution.py:287
  521.4 193.3 %all-to-all-start.4 = ((f32[32,2,2,16,1024]{4,3,2,1,0:T(8,128)}), f32[32,2,2,16,1024]{4,3,2,1,0:T(8,128)}, u32[]{:S(2)}, u32[]{:S(2)}) async-start(f32[32,2,2,16,1024]{4,3,2,1,0:T(8,128)} %square.5), calls=%async_computation.4 | async-start | bytes 16777216 | tf_op jit(solution)/shard_map/all_to_all | solution.py:287
  714.8 99.4 %all-to-all-start.3 = ((f32[32,2,2,8,1024]{4,3,2,1,0:T(8,128)}), f32[32,2,2,8,1024]{4,3,2,1,0:T(8,128)}, u32[]{:S(2)}, u32[]{:S(2)}) async-start(f32[32,2,2,8,1024]{4,3,2,1,0:T(8,128)} %square.3), calls=%async_computation.3 | async-start | bytes 8388608 | tf_op jit(solution)/shard_map/all_to_all | solution.py:287

commit v2 on v1

--- a/solution.py
+++ b/solution.py
@@ -12,8 +12,8 @@
 
 AXES = ("res", "blk")
 ROWS = 8
-UNITS = 4
-TILE = 256
+UNITS = 8
+TILE = 512
 VMEM = 60 * 1024 * 1024
 
 
@@ -42,24 +42,34 @@
 
 def columns(ref, part, first, lanes, own, high):
     stride = ref.shape[1] // high
-    starts = [(first + i) * own + pl.program_id(1) for i in range(lanes)]
+    starts = [(first + i) * own + pl.program_id(0) for i in range(lanes)]
     return [(part, pl.ds(start, high, stride=stride)) for start in starts]
 
 
-def forward_kernel(tile, own, x_ref, m_ref, w_ref, t_ref, o_ref, l_ref):
+def forward_kernel(tile, own, x_ref, m_ref, w_ref, t_ref, o_ref, f_ref, l_ref):
     high, low = m_ref.shape[3], t_ref.shape[3]
     rows = m_ref.shape[2] // 2
     lanes = tile // 128
 
+    def column(j):
+        return pl.ds(pl.multiple_of(j * tile, tile), tile)
+
+    @pl.when(pl.program_id(1) == 0)
+    def _():
+        def field(j, _):
+            for part in range(2):
+                for i, (p, r) in enumerate(columns(x_ref, part, j * lanes, lanes, own, high)):
+                    at = pl.ds(pl.multiple_of(j * tile, tile) + i * 128, 128)
+                    f_ref[0, part, :, at], f_ref[1, part, :, at] = split(x_ref[p, r, :])
+            return 0
+
+        lax.fori_loop(0, low // tile, field, 0)
+
     def first(j, _):
-        at = pl.ds(pl.multiple_of(j * tile, tile), tile)
+        at = column(j)
         m = (m_ref[0, 0], m_ref[0, 1])
-        real, imag = [
-            dot3(m, split(jnp.concatenate(
-                [x_ref[p, r, :] for p, r in columns(x_ref, part, j * lanes, lanes, own, high)], axis=1
-            )))
-            for part in range(2)
-        ]
+        real = dot3(m, (f_ref[0, 0, :, at], f_ref[1, 0, :, at]))
+        imag = dot3(m, (f_ref[0, 1, :, at], f_ref[1, 1, :, at]))
         re, im = real[:rows] - imag[rows:], imag[:rows] + real[rows:]
         cos, sin = w_ref[0, 0, :, at], w_ref[0, 1, :, at]
         l_ref[0, :rows, at], l_ref[1, :rows, at] = split(re * cos - im * sin)
@@ -67,7 +77,7 @@
         return 0
 
     def second(j, _):
-        at = pl.ds(pl.multiple_of(j * tile, tile), tile)
+        at = column(j)
         value = (l_ref[0], l_ref[1])
         by_cos = dot3(value, (t_ref[0, 0, :, at], t_ref[0, 1, :, at]))
         by_sin = dot3(value, (t_ref[1, 0, :, at], t_ref[1, 1, :, at]))
@@ -80,7 +90,7 @@
     lax.fori_loop(0, low // tile, second, 0)
 
 
-def inverse_kernel(tile, own, units, x_ref, m_ref, w_ref, t_ref, *rest):
+def inverse_kernel(tile, own, units, final, x_ref, m_ref, w_ref, t_ref, *rest):
     a_ref, o_ref, l_ref = rest if len(rest) == 3 else (None, *rest)
     high, low = m_ref.shape[2], t_ref.shape[3]
     rows = x_ref.shape[0] * ROWS
@@ -101,12 +111,15 @@
         real = dot3(m, split(jnp.concatenate([re, im], axis=0)))
         imag = dot3(m, split(jnp.concatenate([im, -re], axis=0)))
         for part, value in enumerate((real, imag)):
-            for i, (p, r) in enumerate(columns(o_ref, part, j * lanes, lanes, own, high)):
-                now = value[:, i * 128:(i + 1) * 128]
-                before = 0.0 if a_ref is None else a_ref[p, r, :]
-                if units > 1:
-                    before = jnp.where(pl.program_id(0) == 0, before, o_ref[p, r, :])
-                o_ref[p, r, :] = now + before
+            before = 0.0 if a_ref is None else a_ref[part, 0, :, at]
+            if units > 1:
+                before = jnp.where(pl.program_id(1) == 0, before, o_ref[part, 0, :, at])
+            value = value + before
+            if final:
+                for i, (p, r) in enumerate(columns(o_ref, part, j * lanes, lanes, own, high)):
+                    o_ref[p, r, :] = value[:, i * 128:(i + 1) * 128]
+            else:
+                o_ref[part, 0, :, at] = value
         return 0
 
     lax.fori_loop(0, low // tile, column, 0)
@@ -155,8 +168,9 @@
     return [done[i % 4][i // 4] for i in range(n)]
 
 
-def square_kernel(blocks, start, scale, x_ref, o_ref):
+def square_kernel(blocks, start, scale, x_ref, *rest):
     sign = (1 - 2 * ((start + pl.program_id(0)) % 2)).astype(jnp.float32)
+    o_ref = rest[-1]
     owners, own = x_ref.shape[:2]
     count = owners * own
     half = count // 2
@@ -197,10 +211,7 @@
         before = now
 
 
-def on_device(modes):
-    own, width = modes.shape[1:]
-    blocks = lax.axis_size("blk")
-    devices = blocks * lax.axis_size("res")
+def plan(own, width, devices, blocks):
     units = UNITS
     while units > 2 and width // (devices * ROWS * units // 2) < 128:
         units //= 2
@@ -223,15 +234,16 @@
     ]
 
     once = pl.Buffered(1)
-    tables = pl.BlockSpec(low_tables.shape, lambda u, e: (0, 0, 0, 0), pipeline_mode=once)
-    field = (2, own * width // 128, 128)
-    fields = pl.BlockSpec(field, lambda u, e: (0, 0, 0), pipeline_mode=once)
-    packet = pl.BlockSpec((devices, 1, 2, ROWS, low), lambda u, e: (0, e, 0, u, 0))
+    tables = pl.BlockSpec(low_tables.shape, lambda e, u: (0, 0, 0, 0), pipeline_mode=once)
+    woven = (2, own * width // 128, 128)
+    plain = (2, own, high, low)
+    plains = pl.BlockSpec((2, 1, high, low), lambda e, u: (0, e, 0, 0))
+    packet = pl.BlockSpec((devices, 1, 2, ROWS, low), lambda e, u: (0, e, 0, u, 0))
     params = pltpu.CompilerParams(vmem_limit_bytes=VMEM)
-    scratch = [pltpu.VMEM((2, 2 * rows, low), jnp.bfloat16)]
+    sums = pltpu.VMEM((2, 2 * rows, low), jnp.bfloat16)
 
     def of_unit(start, table):
-        return pl.BlockSpec((1, *table.shape[1:]), lambda u, e: (start + u, 0, 0, 0))
+        return pl.BlockSpec((1, *table.shape[1:]), lambda e, u: (start + u, 0, 0, 0))
 
     def message(count):
         return jax.ShapeDtypeStruct((devices, own, 2, count * ROWS, low), jnp.float32)
@@ -240,68 +252,93 @@
         flops = count * own * 3 * 8 * rows * low * (high + low)
         return pl.CostEstimate(flops=flops, bytes_accessed=8 * own * width, transcendentals=0)
 
-    def forward(start, count, field_in):
+    def forward(start, count, modes):
+        field = modes.reshape(2, own, width // 128, 128).transpose(0, 2, 1, 3).reshape(woven)
         return pl.pallas_call(
             functools.partial(forward_kernel, tile, own),
             out_shape=message(count),
-            grid=(count, own),
-            in_specs=[fields, of_unit(start, befores), of_unit(start, twiddles), tables],
+            grid=(own, count),
+            in_specs=[
+                pl.BlockSpec(woven, lambda e, u: (0, 0, 0), pipeline_mode=once),
+                of_unit(start, befores),
+                of_unit(start, twiddles),
+                tables,
+            ],
             out_specs=packet,
-            scratch_shapes=scratch,
+            scratch_shapes=[pltpu.VMEM((2, 2, high, low), jnp.bfloat16), sums],
             compiler_params=params,
             cost_estimate=cost(count),
             name="forward",
-        )(field_in, befores, twiddles, low_tables)
-
-    def inverse(start, count, packets, total):
+        )(field, befores, twiddles, low_tables)
+
+    def inverse(start, count, packets, total, final):
         extra = [] if total is None else [total]
-        return pl.pallas_call(
-            functools.partial(inverse_kernel, tile, own, count),
-            out_shape=jax.ShapeDtypeStruct(field, jnp.float32),
-            grid=(count, own),
-            in_specs=[packet, of_unit(start, afters), of_unit(start, twiddles), tables, *([fields] * len(extra))],
-            out_specs=pl.BlockSpec(field, lambda u, e: (0, 0, 0)),
-            scratch_shapes=scratch,
+        out = pl.pallas_call(
+            functools.partial(inverse_kernel, tile, own, count, final),
+            out_shape=jax.ShapeDtypeStruct(woven if final else plain, jnp.float32),
+            grid=(own, count),
+            in_specs=[packet, of_unit(start, afters), of_unit(start, twiddles), tables, *([plains] * len(extra))],
+            out_specs=pl.BlockSpec(woven, lambda e, u: (0, 0, 0)) if final else plains,
+            scratch_shapes=[sums],
             compiler_params=params,
             cost_estimate=cost(count),
             name="inverse",
         )(packets, afters, twiddles, low_tables, *extra)
-
-    def square(start, offset, count, packets):
-        def lanes(skip):
-            return pl.BlockSpec((devices, own, 2, ROWS, 128), lambda u, j: (0, 0, 0, skip + u, j))
+        if not final:
+            return out
+        return out.reshape(2, width // 128, own, 128).transpose(0, 2, 1, 3).reshape(2, own, width)
+
+    def square(start, skip, count, packets, into, offset, room):
+        def lanes(first):
+            return pl.BlockSpec((devices, own, 2, ROWS, 128), lambda u, j: (0, 0, 0, first + u, j))
 
         scale = 1.0 / (3 * devices * own * width)
+        extra = [] if into is None else [into]
         return pl.pallas_call(
-            functools.partial(square_kernel, blocks, start + offset, scale),
-            out_shape=message(count),
+            functools.partial(square_kernel, blocks, start, scale),
+            out_shape=message(room),
             grid=(count, low // 128),
-            in_specs=[lanes(offset)],
-            out_specs=lanes(0),
+            in_specs=[lanes(skip), *([pl.BlockSpec(memory_space=pl.ANY)] * len(extra))],
+            out_specs=lanes(offset),
+            input_output_aliases={1: 0} if extra else {},
             compiler_params=params,
             cost_estimate=cost(count),
             name="square",
-        )(packets)
+        )(packets, *extra)
+
+    return units, forward, square, inverse
+
+
+def cuts(units):
+    if units >= 8:
+        return [0, units // 8, units // 2, units], [0, units // 2, units - 1, units]
+    return [0, 1, units], sorted({0, 1, units - 1, units})
+
+
+def on_device(modes):
+    own, width = modes.shape[1:]
+    blocks = lax.axis_size("blk")
+    devices = blocks * lax.axis_size("res")
+    units, forward, square, inverse = plan(own, width, devices, blocks)
+    there, back = cuts(units)
 
     def exchange(packets):
         return lax.all_to_all(packets, AXES, split_axis=0, concat_axis=0, tiled=True)
 
-    field_in = modes.reshape(2, own, width // 128, 128).transpose(0, 2, 1, 3).reshape(field)
-    rest = units - 1
-    first = exchange(forward(0, 1, field_in))
-    second = exchange(forward(1, rest, field_in))
-    home = exchange(square(0, 0, 1, first))
-    if rest > 1:
-        middle = exchange(square(1, 0, rest - 1, second))
-    last = square(1, rest - 1, 1, second)
-    total = inverse(0, 1, home, None)
-    last, total = lax.optimization_barrier((last, total))
-    last = exchange(last)
-    if rest > 1:
-        total = inverse(1, rest - 1, middle, total)
-    total = inverse(rest, 1, last, total)
-    total = total.reshape(2, width // 128, own, 128).transpose(0, 2, 1, 3)
-    return total.reshape(2, own, width)
+    arrived = [(a, b, exchange(forward(a, b - a, modes))) for a, b in zip(there, there[1:])]
+    homes, total = [], None
+    for a, b in zip(back, back[1:]):
+        packets = None
+        for c, d, values in arrived:
+            start, end = max(a, c), min(b, d)
+            if start < end:
+                packets = square(start, start - c, end - start, values, packets, start - a, b - a)
+        if len(homes) >= 2:
+            total = inverse(*homes[-2], total, False)
+            packets, total = lax.optimization_barrier((packets, total))
+        homes.append((a, b - a, exchange(packets)))
+    total = inverse(*homes[-2], total, False)
+    return inverse(*homes[-1], total, True)
 
 
 def solution(mesh):

time: 864 us -> 828 us (0.958)
  Pallas kernels: 338 us -> 255 us
  waiting for transfers between devices: 503 us -> 545 us
    pallas_call x6 -> x7, Pallas kernels: 222 us -> 145 us  [the longest x3 104 us: inverse(): pl.pallas_call(functools.partial(inverse_kernel, tile, own, count, final)...]
    all_to_all x5 -> x6, waiting for transfers between devices: 503 us -> 545 us  [exchange(): lax.all_to_all(packets, AXES, split_axis=0, concat_axis=0, tiled=True)]
    pallas_call x2 -> x3, Pallas kernels: 115 us -> 110 us  [forward(): pl.pallas_call(functools.partial(forward_kernel, tile, own), out_shape=me...]
    all_to_all x5 -> x6, starting transfers between devices: 22.2 us -> 25.2 us  [exchange(): lax.all_to_all(packets, AXES, split_axis=0, concat_axis=0, tiled=True)]
  transfers between devices with their start and end apart: 5 -> 6, of which waited for: 5 -> 6; matrix products, arithmetic and copies ran while one was open for 0% -> 0% of each run, Pallas kernels for 30% -> 27%
where the time goes in v2:
time: 828 us; the launch traced here: 827 us
  waiting for transfers between devices  545 us (66%)
  Pallas kernels  255 us (31%)
  starting transfers between devices  25.2 us (3%)
    all_to_all x6, waiting for transfers between devices, exchange(): lax.all_to_all(packets, AXES, split_axis=0, concat_axis=0, tiled=True)  545 us
    pallas_call x3, Pallas kernels, forward(): pl.pallas_call(functools.partial(forward_kernel, tile, own), out_shape=me...  110 us
    pallas_call x3, Pallas kernels, inverse(): pl.pallas_call(functools.partial(inverse_kernel, tile, own, count, final)...  104 us
    pallas_call x4, Pallas kernels, square(): pl.pallas_call(functools.partial(square_kernel, blocks, start, scale), ou...  40.9 us
    all_to_all x6, starting transfers between devices, exchange(): lax.all_to_all(packets, AXES, split_axis=0, concat_axis=0, tiled=True)  25.2 us
  transfers between devices with their start and end apart: 6, of which 6 were waited for; matrix products, arithmetic and copies ran while one was open for 0% of the time, Pallas kernels for 27%

profile of v2, /device:TPU:0, one launch (start us, length us, event | category | flops | bytes accessed | tf_op | source)
XLA Modules:
  0.0 826.7 jit_solution(13367903920437658153)
XLA Ops:
  0.0 17.7 %forward.5 = f32[32,2,2,8,512]{4,3,2,1,0:T(8,128)} custom-call(f32[2,8192,128]{2,1,0:T(8,128)} %bitcast.10, bf16[8,2,512,1024]{3,2,1,0:T(8,128)(2,1)} %constant.10.clone.m_ref, f32[8,2,256,512]{3,2,1,0:T(8,128)} %constant.9.clone.w_ref, bf16[2,2,512,512]{3,2,1,0:T(8,128)(2,1)} %constant.8.clone.t_ref), custom_call_target="tpu_custom_call" | custom-call | flops 9663676416 | bytes 8388608 | tf_op jit(solution)/shard_map/forward/pallas_call | solution.py:257
  17.7 7.3 all-to-all-start.2
  25.0 40.9 %forward.4 = f32[32,2,2,24,512]{4,3,2,1,0:T(8,128)} custom-call(f32[2,8192,128]{2,1,0:T(8,128)} %bitcast.11, bf16[8,2,512,1024]{3,2,1,0:T(8,128)(2,1)} %constant.10.clone.m_ref, f32[8,2,256,512]{3,2,1,0:T(8,128)} %constant.9.clone.w_ref, bf16[2,2,512,512]{3,2,1,0:T(8,128)(2,1)} %constant.8.clone.t_ref), custom_call_target="tpu_custom_call" | custom-call | flops 28991029248 | bytes 8388608 | tf_op jit(solution)/shard_map/forward/pallas_call | solution.py:257
  65.8 9.2 %all-to-all-done.2.x_ref = f32[32,2,2,8,512]{4,3,2,1,0:T(8,128)S(1)} async-done(((f32[32,2,2,8,512]{4,3,2,1,0:T(8,128)}), f32[32,2,2,8,512]{4,3,2,1,0:T(8,128)S(1)}, u32[]{:S(2)}, u32[]{:S(2)}) %all-to-all-start.2) | async-done | bytes 2097184 | tf_op jit(solution)/shard_map/all_to_all | solution.py:326
  75.0 0.0 copy-start.1
  75.0 3.9 all-to-all-start.1
  79.0 51.4 %forward.3 = f32[32,2,2,32,512]{4,3,2,1,0:T(8,128)} custom-call(f32[2,8192,128]{2,1,0:T(8,128)} %bitcast.12, bf16[8,2,512,1024]{3,2,1,0:T(8,128)(2,1)} %constant.10.clone.m_ref, f32[8,2,256,512]{3,2,1,0:T(8,128)} %constant.9.clone.w_ref, bf16[2,2,512,512]{3,2,1,0:T(8,128)(2,1)} %constant.8.clone.t_ref), custom_call_target="tpu_custom_call" | custom-call | flops 38654705664 | bytes 8388608 | tf_op jit(solution)/shard_map/forward/pallas_call | solution.py:257
  130.3 0.0 copy-done.1
  130.3 90.9 %all-to-all-done.1.x_ref = f32[32,2,2,24,512]{4,3,2,1,0:T(8,128)} async-done(((f32[32,2,2,24,512]{4,3,2,1,0:T(8,128)}), f32[32,2,2,24,512]{4,3,2,1,0:T(8,128)}, u32[]{:S(2)}, u32[]{:S(2)}) %all-to-all-start.1) | async-done | bytes 6291488 | tf_op jit(solution)/shard_map/all_to_all | solution.py:326
  221.3 3.7 all-to-all-start
  225.0 5.8 square.5.rest_0_
  230.8 14.6 %square.6 = f32[32,2,2,32,512]{4,3,2,1,0:T(8,128)} custom-call(f32[32,2,2,24,512]{4,3,2,1,0:T(8,128)} %all-to-all-done.1.x_ref, f32[32,2,2,32,512]{4,3,2,1,0:T(8,128)} %square.5.rest_0_), custom_call_target="tpu_custom_call", output_to_operand_aliasing={{}: (1, {})} | custom-call | flops 28991029248 | bytes 8388608 | tf_op jit(solution)/shard_map/square/pallas_call | solution.py:297
  245.4 169.2 %all-to-all-done.x_ref = f32[32,2,2,32,512]{4,3,2,1,0:T(8,128)} async-done(((f32[32,2,2,32,512]{4,3,2,1,0:T(8,128)}), f32[32,2,2,32,512]{4,3,2,1,0:T(8,128)}, u32[]{:S(2)}, u32[]{:S(2)}) %all-to-all-start) | async-done | bytes 8388640 | tf_op jit(solution)/shard_map/all_to_all | solution.py:326
  414.6 3.7 all-to-all-start.3
  418.3 14.6 %square.7 = f32[32,2,2,24,512]{4,3,2,1,0:T(8,128)} custom-call(f32[32,2,2,32,512]{4,3,2,1,0:T(8,128)} %all-to-all-done.x_ref), custom_call_target="tpu_custom_call" | custom-call | flops 28991029248 | bytes 8388608 | tf_op jit(solution)/shard_map/square/pallas_call | solution.py:297
  432.9 175.0 %all-to-all-done.3.x_ref = f32[32,2,2,32,512]{4,3,2,1,0:T(8,128)} async-done(((f32[32,2,2,32,512]{4,3,2,1,0:T(8,128)}), f32[32,2,2,32,512]{4,3,2,1,0:T(8,128)}, u32[]{:S(2)}, u32[]{:S(2)}) %all-to-all-start.3) | async-done | bytes 8388640 | tf_op jit(solution)/shard_map/all_to_all | solution.py:326
  607.9 3.8 all-to-all-start.5
  611.8 5.9 square.4
  617.6 47.8 %inverse.3.rest_0_ = f32[2,2,1024,512]{3,2,1,0:T(8,128)} custom-call(f32[32,2,2,32,512]{4,3,2,1,0:T(8,128)} %all-to-all-done.3.x_ref, bf16[8,2,1024,512]{3,2,1,0:T(8,128)(2,1)} %constant.11.clone.m_ref, f32[8,2,256,512]{3,2,1,0:T(8,128)} %constant.9.clone.w_ref, bf16[2,2,512,512]{3,2,1,0:T(8,128)(2,1)} %constant.8.clone.t_ref), custom_call_target="tpu_custom_call" | custom-call | flops 38654705664 | bytes 8388608 | tf_op jit(solution)/shard_map/inverse/pallas_call | solution.py:276
  665.5 88.6 %all-to-all-done.5.x_ref = f32[32,2,2,24,512]{4,3,2,1,0:T(8,128)} async-done(((f32[32,2,2,24,512]{4,3,2,1,0:T(8,128)}), f32[32,2,2,24,512]{4,3,2,1,0:T(8,128)}, u32[]{:S(2)}, u32[]{:S(2)}) %all-to-all-start.5) | async-done | bytes 6291488 | tf_op jit(solution)/shard_map/all_to_all | solution.py:326
  754.0 2.7 all-to-all-start.4
  756.8 38.1 %inverse.4.rest_0_ = f32[2,2,1024,512]{3,2,1,0:T(8,128)} custom-call(f32[32,2,2,24,512]{4,3,2,1,0:T(8,128)} %all-to-all-done.5.x_ref, bf16[8,2,1024,512]{3,2,1,0:T(8,128)(2,1)} %constant.11.clone.m_ref, f32[8,2,256,512]{3,2,1,0:T(8,128)} %constant.9.clone.w_ref, bf16[2,2,512,512]{3,2,1,0:T(8,128)(2,1)} %constant.8.clone.t_ref, ...), custom_call_target="tpu_custom_call" | custom-call | flops 28991029248 | bytes 8388608 | tf_op jit(solution)/shard_map/inverse/pallas_call | solution.py:276
  794.9 11.9 %all-to-all-done.4.x_ref = f32[32,2,2,8,512]{4,3,2,1,0:T(8,128)S(1)} async-done(((f32[32,2,2,8,512]{4,3,2,1,0:T(8,128)}), f32[32,2,2,8,512]{4,3,2,1,0:T(8,128)S(1)}, u32[]{:S(2)}, u32[]{:S(2)}) %all-to-all-start.4) | async-done | bytes 2097184 | tf_op jit(solution)/shard_map/all_to_all | solution.py:326
  806.8 0.0 copy-start
  806.8 1.4 copy-done
  808.2 18.5 %inverse.5 = f32[2,8192,128]{2,1,0:T(8,128)} custom-call(f32[32,2,2,8,512]{4,3,2,1,0:T(8,128)} %copy-done, bf16[8,2,1024,512]{3,2,1,0:T(8,128)(2,1)} %constant.11.clone.m_ref, f32[8,2,256,512]{3,2,1,0:T(8,128)} %constant.9.clone.w_ref, bf16[2,2,512,512]{3,2,1,0:T(8,128)(2,1)} %constant.8.clone.t_ref, f32[2,2,1024,512]{3,2,1,0:T(8,128)} %inverse.4.rest_0_), custom_call_target="tpu_custom_call" | custom-call | flops 9663676416 | bytes 8388608 | tf_op jit(solution)/shard_map/inverse/pallas_call | solution.py:276
Async XLA Ops:
  17.7 57.4 %all-to-all-start.2 = ((f32[32,2,2,8,512]{4,3,2,1,0:T(8,128)}), f32[32,2,2,8,512]{4,3,2,1,0:T(8,128)S(1)}, u32[]{:S(2)}, u32[]{:S(2)}) async-start(f32[32,2,2,8,512]{4,3,2,1,0:T(8,128)} %forward.5), calls=%async_computation.2 | async-start | bytes 4194304 | tf_op jit(solution)/shard_map/all_to_all | solution.py:326
  75.0 55.3 %copy-start.1 = (f32[32,2,2,8,512]{4,3,2,1,0:T(8,128)}, f32[32,2,2,8,512]{4,3,2,1,0:T(8,128)S(1)}, u32[]{:S(2)}) copy-start(f32[32,2,2,8,512]{4,3,2,1,0:T(8,128)S(1)} %all-to-all-done.2.x_ref) | copy-start | bytes 6291460
  75.0 146.2 %all-to-all-start.1 = ((f32[32,2,2,24,512]{4,3,2,1,0:T(8,128)}), f32[32,2,2,24,512]{4,3,2,1,0:T(8,128)}, u32[]{:S(2)}, u32[]{:S(2)}) async-start(f32[32,2,2,24,512]{4,3,2,1,0:T(8,128)} %forward.4), calls=%async_computation.1 | async-start | bytes 12582912 | tf_op jit(solution)/shard_map/all_to_all | solution.py:326
  221.3 193.3 %all-to-all-start = ((f32[32,2,2,32,512]{4,3,2,1,0:T(8,128)}), f32[32,2,2,32,512]{4,3,2,1,0:T(8,128)}, u32[]{:S(2)}, u32[]{:S(2)}) async-start(f32[32,2,2,32,512]{4,3,2,1,0:T(8,128)} %forward.3), calls=%async_computation | async-start | bytes 16777216 | tf_op jit(solution)/shard_map/all_to_all | solution.py:326
  414.6 193.3 %all-to-all-start.3 = ((f32[32,2,2,32,512]{4,3,2,1,0:T(8,128)}), f32[32,2,2,32,512]{4,3,2,1,0:T(8,128)}, u32[]{:S(2)}, u32[]{:S(2)}) async-start(f32[32,2,2,32,512]{4,3,2,1,0:T(8,128)} %square.6), calls=%async_computation.3 | async-start | bytes 16777216 | tf_op jit(solution)/shard_map/all_to_all | solution.py:326
  607.9 146.1 %all-to-all-start.5 = ((f32[32,2,2,24,512]{4,3,2,1,0:T(8,128)}), f32[32,2,2,24,512]{4,3,2,1,0:T(8,128)}, u32[]{:S(2)}, u32[]{:S(2)}) async-start(f32[32,2,2,24,512]{4,3,2,1,0:T(8,128)} %square.7), calls=%async_computation.5 | async-start | bytes 12582912 | tf_op jit(solution)/shard_map/all_to_all | solution.py:326
  754.0 52.8 %all-to-all-start.4 = ((f32[32,2,2,8,512]{4,3,2,1,0:T(8,128)}), f32[32,2,2,8,512]{4,3,2,1,0:T(8,128)S(1)}, u32[]{:S(2)}, u32[]{:S(2)}) async-start(f32[32,2,2,8,512]{4,3,2,1,0:T(8,128)} %square.4), calls=%async_computation.4 | async-start | bytes 4194304 | tf_op jit(solution)/shard_map/all_to_all | solution.py:326
  806.8 1.4 copy-start
